TPU v7x, 32 devices: a whole 2x2x4 slice. The times are simulated.
32 devices in a mesh: section: 4 (over z), dp: 8 (over y, x, core).
Axes of the slice: x: 2, y: 2, z: 4, core: 2. Of those that a mesh axis runs over, the one named last changes fastest.
Arguments:
- inject: bfloat16 [4, 64, 4096], P('section', 'dp'), may hold values from -42 to 42, as said below
- w_gate: bfloat16 [4, 4096, 11008], P('section', None, 'dp'), may hold values from -0.09375 to 0.09375
- w_up: bfloat16 [4, 4096, 11008], P('section', None, 'dp'), may hold values from -0.09375 to 0.09375
- w_down: bfloat16 [4, 11008, 4096], P('section', 'dp'), may hold values from -0.0546875 to 0.0546875
- gain: float32 [4, 4096], P('section'), may hold values from 0.5 to 1.5
Outputs:
- iterate: float32 [4, 64, 4096], P('section', 'dp')
- mixing: float32 [4, 5, 5], P('section')
Inputs may be any that keep to these rules, and one draw needn't show every extreme that they name: inject has entries of varied magnitude from token to token.
All inputs are finite; a program needn't handle non-finite values.
Results may differ from a plain program's by a relative error of at most 0.0038.
Values may be sent and summed in bfloat16 or wider, within the bound.
A program may use at most 128 MiB of HBM per device.

v0:
```python
import jax
import jax.numpy as jnp
from jax import lax
from jax.sharding import PartitionSpec as P

ITERS = 5
HIST = 5


def passed_along(array, axis, by):
    peers = lax.axis_size(axis)
    return lax.ppermute(array, axis, [(i, (i + by) % peers) for i in range(peers)])


def rms_scaled(values, gain_row):
    inverse = lax.rsqrt(jnp.mean(values * values, axis=-1, keepdims=True) + 1e-06)
    return (values * inverse * gain_row).astype(jnp.bfloat16)


def solve_small(system, target):
    count = system.shape[-1]
    entries = [[system[..., i, j] for j in range(count)] for i in range(count)]
    values = [target[..., i] for i in range(count)]
    for p in range(count):
        for i in range(p + 1, count):
            factor = entries[i][p] / entries[p][p]
            for j in range(p, count):
                entries[i][j] = entries[i][j] - factor * entries[p][j]
            values[i] = values[i] - factor * values[p]
    answer = [None] * count
    for i in range(count - 1, -1, -1):
        accum = values[i]
        for j in range(i + 1, count):
            accum = accum - entries[i][j] * answer[j]
        answer[i] = accum / entries[i][i]
    return jnp.stack(answer, axis=-1)


def mixing_weights(matrix, iteration):
    live = (jnp.arange(HIST) <= iteration).astype(jnp.float32)
    damp = 0.01 * jnp.trace(matrix) / (iteration + 1) + 1e-06
    eye_mat = jnp.eye(HIST, dtype=jnp.float32)
    diagonal = live * damp + (1.0 - live)
    system = matrix * live[:, None] * live[None, :] + eye_mat * diagonal[None, :]
    beta = solve_small(system, live)
    return beta / jnp.sum(beta)


def local(inject, w_gate, w_up, w_down, gain):
    tok_rows = inject.shape[1]
    features = inject.shape[2]
    groups = lax.axis_size("dp")
    cell_count = float(tok_rows * groups * features)
    source = inject[0].astype(jnp.float32)
    gain_row = gain[0]
    gate_local = w_gate[0]
    up_local = w_up[0]
    down_local = w_down[0]
    iterate = jnp.zeros((tok_rows, features), jnp.float32)
    images = jnp.zeros((HIST, tok_rows, features), jnp.float32)
    misfits = jnp.zeros((HIST, tok_rows, features), jnp.float32)
    gram_matrix = jnp.zeros((HIST, HIST), jnp.float32)
    mixing = jnp.zeros((ITERS, HIST), jnp.float32)
    for iteration in range(ITERS):
        normed = rms_scaled(iterate, gain_row)
        segment = lax.all_gather(normed, "dp", axis=0, tiled=True)
        gate_val = jnp.dot(segment, gate_local, preferred_element_type=jnp.float32)
        up_val = jnp.dot(segment, up_local, preferred_element_type=jnp.float32)
        hidden = (jax.nn.silu(gate_val) * up_val).astype(jnp.bfloat16)
        partials = jnp.dot(hidden, down_local, preferred_element_type=jnp.float32)
        summed = lax.psum_scatter(
            partials.astype(jnp.bfloat16), "dp", scatter_dimension=0, tiled=True
        ).astype(jnp.float32)
        output = (iterate + summed).astype(jnp.bfloat16)
        before = passed_along(output, "section", 1)
        mapped = source + 0.5 * before.astype(jnp.float32)
        misfit = mapped - iterate
        images = images.at[iteration].set(mapped)
        misfits = misfits.at[iteration].set(misfit)
        local_gram = (
            jnp.einsum("htd,gtd->hg", misfits, misfits, precision=lax.Precision.HIGHEST)
            / cell_count
        )
        gram_matrix = lax.psum(local_gram, "dp")
        weights = mixing_weights(gram_matrix, iteration)
        mixing = mixing.at[iteration].set(weights)
        iterate = jnp.einsum("h,htd->td", weights, images, precision=lax.Precision.HIGHEST)
    return (iterate[None], mixing[None])


def solution(mesh):
    placed = (
        P("section", "dp", None),
        P("section", None, "dp"),
        P("section", None, "dp"),
        P("section", "dp", None),
        P("section", None),
    )
    return jax.shard_map(
        local,
        mesh=mesh,
        in_specs=placed,
        out_specs=(P("section", "dp", None), P("section", None, None)),
        check_vma=False,
    )
```

profile of v0, /device:TPU:1, one launch (start us, length us, event | category | flops | bytes accessed | tf_op | source)
XLA Modules:
  0.0 642.4 jit_solution(4416459075443289073)
XLA Ops:
  7.9 11.2 %all_gather.15 = bf16[64,4096]{1,0:T(8,128)(2,1)S(1)} all-gather(bf16[8,4096]{1,0:T(8,128)(2,1)S(1)} %mul.1042), channel_id=1, replica_groups=mesh['section'=4,'dp'=8] {'dp'}, dimensions={0}, use_global_device_ids=true | all-gather | bytes 589824 | tf_op jit(solution)/shard_map/all_gather | solution.py:66
  19.1 7.6 %fusion.28 = f32[64,1376]{1,0:T(8,128)S(1)} fusion(bf16[64,4096]{1,0:T(8,128)(2,1)S(1)} %all_gather.15, bf16[1,4096,1376]{1,2,0:T(8,128)(2,1)} %param.36), kind=kOutput, calls=%fused_computation.28 | convolution fusion | flops 721420288 | bytes 12148736 | tf_op jit(solution)/shard_map/dot_general | solution.py:67
  26.8 14.1 %fusion.30 = bf16[64,4096]{1,0:T(8,128)(2,1)} fusion(bf16[1,1376,4096]{2,1,0:T(8,128)(2,1)} %param.38, bf16[64,4096]{1,0:T(8,128)(2,1)S(1)} %all_gather.15, bf16[1,4096,1376]{1,2,0:T(8,128)(2,1)} %param.37, f32[64,1376]{1,0:T(8,128)S(1)} %fusion.28), kind=kOutput, calls=%fused_computation.30 | convolution fusion | flops 1443631104 | bytes 23945216 | tf_op jit(solution)/shard_map/dot_general | solution.py:70
  41.0 33.4 %reduce-scatter.6.cloned.1.call-done = bf16[8,4096]{1,0:T(8,128)(2,1)} async-done(((bf16[64,4096]{1,0:T(8,128)(2,1)}), bf16[8,4096]{1,0:T(8,128)(2,1)}) %reduce-scatter.6.cloned.1.call-update) | async-done | bytes 65552 | tf_op jit(solution)/shard_map/reduce_scatter | solution.py:71
  76.3 3.2 collective-permute-done
  82.4 13.5 %psum.35 = f32[5,5]{1,0:T(8,128)S(1)} all-reduce(f32[5,5]{1,0:T(8,128)S(1)} %fusion.86), channel_id=1, replica_groups=mesh['section'=4,'dp'=8] {'dp'}, use_global_device_ids=true, to_apply=%region_1.2 | all-reduce | flops 25 | bytes 200 | tf_op jit(solution)/shard_map/psum | solution.py:84
  135.1 10.8 %all_gather.16 = bf16[64,4096]{1,0:T(8,128)(2,1)S(1)} all-gather(bf16[8,4096]{1,0:T(8,128)(2,1)S(1)} %fusion.156), channel_id=1, replica_groups=mesh['section'=4,'dp'=8] {'dp'}, dimensions={0}, use_global_device_ids=true | all-gather | bytes 589824 | tf_op jit(solution)/shard_map/all_gather | solution.py:66
  145.9 7.6 %fusion.26 = f32[64,1376]{1,0:T(8,128)S(1)} fusion(bf16[64,4096]{1,0:T(8,128)(2,1)S(1)} %all_gather.16, bf16[1,4096,1376]{1,2,0:T(8,128)(2,1)} %param.36), kind=kOutput, calls=%fused_computation.26 | convolution fusion | flops 721420288 | bytes 12148736 | tf_op jit(solution)/shard_map/dot_general | solution.py:67
  153.5 14.0 %fusion.33 = bf16[64,4096]{1,0:T(8,128)(2,1)} fusion(bf16[1,1376,4096]{2,1,0:T(8,128)(2,1)} %param.38, bf16[64,4096]{1,0:T(8,128)(2,1)S(1)} %all_gather.16, bf16[1,4096,1376]{1,2,0:T(8,128)(2,1)} %param.37, f32[64,1376]{1,0:T(8,128)S(1)} %fusion.26), kind=kOutput, calls=%fused_computation.31 | convolution fusion | flops 1443631104 | bytes 23945216 | tf_op jit(solution)/shard_map/dot_general | solution.py:70
  167.7 31.3 %reduce-scatter.8.cloned.1.call-done = bf16[8,4096]{1,0:T(8,128)(2,1)} async-done(((bf16[64,4096]{1,0:T(8,128)(2,1)}), bf16[8,4096]{1,0:T(8,128)(2,1)}) %reduce-scatter.8.cloned.1.call-update) | async-done | bytes 65552 | tf_op jit(solution)/shard_map/reduce_scatter | solution.py:71
  201.9 3.0 collective-permute-done.1
  205.0 2.8 fusion.85
  207.8 13.5 %psum.36 = f32[5,5]{1,0:T(8,128)S(1)} all-reduce(f32[5,5]{1,0:T(8,128)S(1)} %fusion.85), channel_id=1, replica_groups=mesh['section'=4,'dp'=8] {'dp'}, use_global_device_ids=true, to_apply=%region_5.6 | all-reduce | flops 25 | bytes 200 | tf_op jit(solution)/shard_map/psum | solution.py:84
  260.4 10.5 %all_gather.17 = bf16[64,4096]{1,0:T(8,128)(2,1)S(1)} all-gather(bf16[8,4096]{1,0:T(8,128)(2,1)S(1)} %fusion.152), channel_id=1, replica_groups=mesh['section'=4,'dp'=8] {'dp'}, dimensions={0}, use_global_device_ids=true | all-gather | bytes 589824 | tf_op jit(solution)/shard_map/all_gather | solution.py:66
  270.9 7.6 %fusion.24 = f32[64,1376]{1,0:T(8,128)S(1)} fusion(bf16[64,4096]{1,0:T(8,128)(2,1)S(1)} %all_gather.17, bf16[1,4096,1376]{1,2,0:T(8,128)(2,1)} %param.36), kind=kOutput, calls=%fused_computation.24 | convolution fusion | flops 721420288 | bytes 12148736 | tf_op jit(solution)/shard_map/dot_general | solution.py:67
  278.5 14.0 %fusion.36 = bf16[64,4096]{1,0:T(8,128)(2,1)} fusion(bf16[1,1376,4096]{2,1,0:T(8,128)(2,1)} %param.38, bf16[64,4096]{1,0:T(8,128)(2,1)S(1)} %all_gather.17, bf16[1,4096,1376]{1,2,0:T(8,128)(2,1)} %param.37, f32[64,1376]{1,0:T(8,128)S(1)} %fusion.24), kind=kOutput, calls=%fused_computation.32 | convolution fusion | flops 1443631104 | bytes 23945216 | tf_op jit(solution)/shard_map/dot_general | solution.py:70
  292.6 31.3 %reduce-scatter.10.cloned.1.call-done = bf16[8,4096]{1,0:T(8,128)(2,1)} async-done(((bf16[64,4096]{1,0:T(8,128)(2,1)}), bf16[8,4096]{1,0:T(8,128)(2,1)}) %reduce-scatter.10.cloned.1.call-update) | async-done | bytes 65552 | tf_op jit(solution)/shard_map/reduce_scatter | solution.py:71
  326.8 3.0 collective-permute-done.2
  332.8 13.5 %psum.37 = f32[5,5]{1,0:T(8,128)S(1)} all-reduce(f32[5,5]{1,0:T(8,128)S(1)} %fusion.84), channel_id=1, replica_groups=mesh['section'=4,'dp'=8] {'dp'}, use_global_device_ids=true, to_apply=%region_9.10 | all-reduce | flops 25 | bytes 200 | tf_op jit(solution)/shard_map/psum | solution.py:84
  385.3 10.5 %all_gather.18 = bf16[64,4096]{1,0:T(8,128)(2,1)S(1)} all-gather(bf16[8,4096]{1,0:T(8,128)(2,1)S(1)} %fusion.148), channel_id=1, replica_groups=mesh['section'=4,'dp'=8] {'dp'}, dimensions={0}, use_global_device_ids=true | all-gather | bytes 589824 | tf_op jit(solution)/shard_map/all_gather | solution.py:66
  395.8 7.6 %fusion.22 = f32[64,1376]{1,0:T(8,128)S(1)} fusion(bf16[64,4096]{1,0:T(8,128)(2,1)S(1)} %all_gather.18, bf16[1,4096,1376]{1,2,0:T(8,128)(2,1)} %param.36), kind=kOutput, calls=%fused_computation.22 | convolution fusion | flops 721420288 | bytes 12148736 | tf_op jit(solution)/shard_map/dot_general | solution.py:67
  403.5 14.0 %fusion.39 = bf16[64,4096]{1,0:T(8,128)(2,1)} fusion(bf16[1,1376,4096]{2,1,0:T(8,128)(2,1)} %param.38, bf16[64,4096]{1,0:T(8,128)(2,1)S(1)} %all_gather.18, bf16[1,4096,1376]{1,2,0:T(8,128)(2,1)} %param.37, f32[64,1376]{1,0:T(8,128)S(1)} %fusion.22), kind=kOutput, calls=%fused_computation.33 | convolution fusion | flops 1443631104 | bytes 23945216 | tf_op jit(solution)/shard_map/dot_general | solution.py:70
  418.3 30.7 %reduce-scatter.12.cloned.1.call-done = bf16[8,4096]{1,0:T(8,128)(2,1)} async-done(((bf16[64,4096]{1,0:T(8,128)(2,1)}), bf16[8,4096]{1,0:T(8,128)(2,1)}) %reduce-scatter.12.cloned.1.call-update) | async-done | bytes 65552 | tf_op jit(solution)/shard_map/reduce_scatter | solution.py:71
  451.2 3.7 collective-permute-done.3
  455.0 2.8 fusion.83
  457.8 13.5 %psum.38 = f32[5,5]{1,0:T(8,128)S(1)} all-reduce(f32[5,5]{1,0:T(8,128)S(1)} %fusion.83), channel_id=1, replica_groups=mesh['section'=4,'dp'=8] {'dp'}, use_global_device_ids=true, to_apply=%region_13.14 | all-reduce | flops 25 | bytes 200 | tf_op jit(solution)/shard_map/psum | solution.py:84
  509.8 10.6 %all_gather.19 = bf16[64,4096]{1,0:T(8,128)(2,1)S(1)} all-gather(bf16[8,4096]{1,0:T(8,128)(2,1)S(1)} %fusion.144), channel_id=1, replica_groups=mesh['section'=4,'dp'=8] {'dp'}, dimensions={0}, use_global_device_ids=true | all-gather | bytes 589824 | tf_op jit(solution)/shard_map/all_gather | solution.py:66
  520.4 7.6 %fusion.20 = f32[64,1376]{1,0:T(8,128)S(1)} fusion(bf16[64,4096]{1,0:T(8,128)(2,1)S(1)} %all_gather.19, bf16[1,4096,1376]{1,2,0:T(8,128)(2,1)} %param.36), kind=kOutput, calls=%fused_computation.20 | convolution fusion | flops 721420288 | bytes 12148736 | tf_op jit(solution)/shard_map/dot_general | solution.py:67
  528.0 14.0 %fusion.42 = bf16[64,4096]{1,0:T(8,128)(2,1)} fusion(bf16[1,1376,4096]{2,1,0:T(8,128)(2,1)} %param.38, bf16[64,4096]{1,0:T(8,128)(2,1)S(1)} %all_gather.19, bf16[1,4096,1376]{1,2,0:T(8,128)(2,1)} %param.37, f32[64,1376]{1,0:T(8,128)S(1)} %fusion.20), kind=kOutput, calls=%fused_computation.34 | convolution fusion | flops 1443631104 | bytes 23945216 | tf_op jit(solution)/shard_map/dot_general | solution.py:70
  543.2 30.3 %reduce-scatter.14.cloned.1.call-done = bf16[8,4096]{1,0:T(8,128)(2,1)} async-done(((bf16[64,4096]{1,0:T(8,128)(2,1)}), bf16[8,4096]{1,0:T(8,128)(2,1)}) %reduce-scatter.14.cloned.1.call-update) | async-done | bytes 65552 | tf_op jit(solution)/shard_map/reduce_scatter | solution.py:71
  575.7 3.7 collective-permute-done.4
  582.3 13.5 %psum.39 = f32[5,5]{1,0:T(8,128)S(1)} all-reduce(f32[5,5]{1,0:T(8,128)S(1)} %fusion.82), channel_id=1, replica_groups=mesh['section'=4,'dp'=8] {'dp'}, use_global_device_ids=true, to_apply=%region_17.18 | all-reduce | flops 25 | bytes 200 | tf_op jit(solution)/shard_map/psum | solution.py:84
  (110 shorter events, 44.0 us)
Async XLA Ops:
  7.2 67.2 %reduce-scatter.6.cloned.1.call-start = ((), (), s32[]{:S(2)}) async-start(), calls=%async_computation.5 | async-start | bytes 589824 | tf_op jit(solution)/shard_map/reduce_scatter | solution.py:71
  26.8 52.7 %copy-start = (bf16[1,8,4096]{2,1,0:T(8,128)(2,1)S(1)}, bf16[1,8,4096]{2,1,0:T(8,128)(2,1)}, u32[]{:S(2)}) copy-start(bf16[1,8,4096]{2,1,0:T(8,128)(2,1)} %param.35) | copy-start | bytes 196612
  26.8 108.2 %copy-start.1 = (f32[1,4096]{1,0:T(1,128)S(1)}, f32[1,4096]{1,0:T(1,128)}, u32[]{:S(2)}) copy-start(f32[1,4096]{1,0:T(1,128)} %param.39) | copy-start | bytes 49156
  40.9 158.1 %reduce-scatter.8.cloned.1.call-start = ((), (), s32[]{:S(2)}) async-start(), calls=%async_computation.6 | async-start | bytes 589824 | tf_op jit(solution)/shard_map/reduce_scatter | solution.py:71
  74.4 5.1 collective-permute-start
  167.6 156.4 %reduce-scatter.10.cloned.1.call-start = ((), (), s32[]{:S(2)}) async-start(), calls=%async_computation.7 | async-start | bytes 589824 | tf_op jit(solution)/shard_map/reduce_scatter | solution.py:71
  199.9 5.0 collective-permute-start.1
  292.6 156.4 %reduce-scatter.12.cloned.1.call-start = ((), (), s32[]{:S(2)}) async-start(), calls=%async_computation.8 | async-start | bytes 589824 | tf_op jit(solution)/shard_map/reduce_scatter | solution.py:71
  324.9 5.0 collective-permute-start.2
  417.6 155.9 %reduce-scatter.14.cloned.1.call-start = ((), (), s32[]{:S(2)}) async-start(), calls=%async_computation.9 | async-start | bytes 589824 | tf_op jit(solution)/shard_map/reduce_scatter | solution.py:71
  449.9 5.0 collective-permute-start.3
  574.4 5.0 collective-permute-start.4
Sparse Core Ops, SparseCore 0:
  41.0 33.3 reduce-scatter.5
  167.7 31.2 reduce-scatter.7
  292.7 31.2 reduce-scatter.9
  417.7 31.2 reduce-scatter.11
  542.2 31.2 reduce-scatter.13
where the time goes:
time: 654 us; the launch traced here: 642 us
  between operations  189 us (29%)
  waiting for transfers between devices  174 us (27%)
  matrix products  129 us (20%)
  blocking collectives  121 us (19%)
  local copies, waits for them, and re-layouts  12.7 us (2%)
  other arithmetic  9.55 us (1%)
    reduce_scatter x5, waiting for transfers between devices, local(): lax.psum_scatter(partials.astype(jnp.bfloat16), 'dp', scatter_dimension=0...  157 us
    dot_general x5, matrix products, local(): partials = jnp.dot(hidden, down_local, preferred_element_type=jnp.float32)  70.2 us
    psum x5, blocking collectives, local(): gram_matrix = lax.psum(local_gram, 'dp')  67.6 us
    all_gather x5, blocking collectives, local(): segment = lax.all_gather(normed, 'dp', axis=0, tiled=True)  53.6 us
    dot_general x5, matrix products, local(): gate_val = jnp.dot(segment, gate_local, preferred_element_type=jnp.float32)  38.2 us
    ppermute x5, waiting for transfers between devices, passed_along(): lax.ppermute(array, axis, [(i, (i + by) % peers) for i in range(peers)])  16.6 us
    dot_general x5, matrix products, local(): jnp.einsum('htd,gtd->hg', misfits, misfits, precision=lax.Precision.HIGHEST)  14.2 us
  transfers between devices with their start and end apart: 10, of which 10 were waited for; matrix products, arithmetic and copies ran while one was open for 1% of the time, Pallas kernels for 0%

commit v1 on v0

v1 whole, which is shorter than its diff:
```python
import functools

import jax
import jax.numpy as jnp
from jax import lax
from jax.experimental import pallas as pl
from jax.experimental.pallas import tpu as pltpu
from jax.sharding import PartitionSpec as P

ITERS = 5
HIST = 5
MESH = pl.DeviceIdType.MESH
F32 = jnp.float32
BF16 = jnp.bfloat16
ROW_CUTS = 4


def solve_small(entries, values):
    count = len(values)
    for p in range(count):
        for i in range(p + 1, count):
            factor = entries[i][p] / entries[p][p]
            for j in range(p, count):
                entries[i][j] = entries[i][j] - factor * entries[p][j]
            values[i] = values[i] - factor * values[p]
    answer = [None] * count
    for i in range(count - 1, -1, -1):
        accum = values[i]
        for j in range(i + 1, count):
            accum = accum - entries[i][j] * answer[j]
        answer[i] = accum / entries[i][i]
    return answer


def kernel(
    n_sec, n_dp,
    inj_ref, gate_hbm, up_hbm, down_hbm, gain_ref,
    out_ref, mix_ref,
    w_gate, w_up, w_down,
    inj_all, inj, x, xg, inv, hidden,
    outs, misfits, acc, gram,
    pair_send, pair_recv, pair_mine, rs_send, rs_recv, out_send, mix_s,
    w_sem, inj_ssem, inj_rsem, pair_ssem, pair_rsem, rs_ssem, rs_rsem,
    z_ssem, ag_ssem, ag_rsem,
):
    sec = lax.axis_index("section")
    me = lax.axis_index("dp")
    chips = n_dp // 2
    chip = me // 2
    core = me % 2
    other = chip * 2 + 1 - core
    rows, feats = inj_ref.shape
    tokens = inj.shape[0]
    block = feats // n_dp
    hid = hidden.shape[1]
    after = (sec + 1) % n_sec
    before = (sec + n_sec - 1) % n_sec

    def cols(b):
        return pl.ds(pl.multiple_of(b * block, block), block)

    def remote(src, dst, ssem, rsem, device):
        return pltpu.make_async_remote_copy(
            src_ref=src, dst_ref=dst, send_sem=ssem, recv_sem=rsem,
            device_id=device, device_id_type=MESH,
        )

    def weight_copies(which):
        copies = []
        for a in which:
            src, dst = ((gate_hbm, w_gate), (up_hbm, w_up), (down_hbm, w_down))[a]
            size = dst.shape[0]
            edges = [size * c // ROW_CUTS // 32 * 32 for c in range(ROW_CUTS)] + [size]
            for c in range(ROW_CUTS):
                part = pl.ds(edges[c], edges[c + 1] - edges[c])
                copies.append(
                    pltpu.make_async_copy(src.at[0, part], dst.at[part], w_sem.at[a, c])
                )
        return copies

    for copy in weight_copies((0, 1, 2)):
        copy.start()

    barrier = pltpu.get_barrier_semaphore()
    for off in range(1, n_dp):
        pl.semaphore_signal(barrier, inc=1, device_id=(sec, (me + off) % n_dp), device_id_type=MESH)
    pl.semaphore_signal(barrier, inc=1, device_id=(after, me), device_id_type=MESH)
    pl.semaphore_signal(barrier, inc=1, device_id=(before, me), device_id_type=MESH)
    pl.semaphore_wait(barrier, n_dp + 1)

    def inject_copy(off):
        return remote(
            inj_ref, inj_all.at[me], inj_ssem.at[off], inj_rsem.at[me],
            (sec, (me + off) % n_dp),
        )

    for off in range(1, n_dp):
        inject_copy(off).start()

    gram[...] = jnp.zeros_like(gram)
    acc[...] = jnp.zeros_like(acc)

    inj[pl.ds(pl.multiple_of(me * rows, rows), rows), :] = inj_ref[...].astype(F32)
    for off in range(1, n_dp):
        peer = (me + n_dp - off) % n_dp
        remote(
            inj_ref, inj_all.at[peer], inj_ssem.at[off], inj_rsem.at[peer], (sec, peer)
        ).wait_recv()
        inj[pl.ds(pl.multiple_of(peer * rows, rows), rows), :] = inj_all[peer].astype(F32)

    def fold(values):
        return jnp.sum(values.reshape(tokens // 8, 8, block), axis=0)

    def add_gram(k, b):
        def one(j, carry):
            acc[j] = acc[j] + fold(misfits[k, :, cols(b)] * misfits[j, :, cols(b)])
            return carry

        lax.fori_loop(0, k + 1, one, 0)

    def finish(k):
        for j in range(HIST):
            total = jnp.sum(jnp.sum(acc[j], axis=0, keepdims=True), axis=1, keepdims=True)
            value = jnp.broadcast_to(total / float(tokens * feats), (8, 128))
            gram[k, j] = value
            gram[j, k] = value
        acc[...] = jnp.zeros_like(acc)
        live = [jnp.where(i <= k, 1.0, 0.0).astype(F32) for i in range(HIST)]
        trace = gram[0, 0]
        for i in range(1, HIST):
            trace = trace + gram[i, i]
        damp = 0.01 * trace / jnp.full((8, 128), k + 1, jnp.int32).astype(F32) + 1e-06
        system = [
            [
                gram[i, j] * (live[i] * live[j])
                + ((live[i] * damp + (1.0 - live[i])) if i == j else 0.0)
                for j in range(HIST)
            ]
            for i in range(HIST)
        ]
        beta = solve_small(system, [jnp.full((8, 128), live[i], F32) for i in range(HIST)])
        whole = beta[0]
        for i in range(1, HIST):
            whole = whole + beta[i]
        scale = jnp.float32(0.0)
        for i in range(HIST):
            weight = (beta[i] / whole)[0, 0]
            mix_ref[k, i] = weight
            mix_s[i] = weight
            scale = scale + weight

        def one(b, square):
            def slot(i, value):
                return value + (0.5 * mix_s[i]) * outs[i - 1, b].astype(F32)

            value = lax.fori_loop(1, k + 1, slot, scale * inj[:, cols(b)])
            x[:, cols(b)] = value
            xg[:, cols(b)] = (value * gain_ref[:, cols(b)]).astype(BF16)
            squared = value * value
            for g in range(block // 128):
                square = square + squared[:, g * 128 : (g + 1) * 128]
            return square

        square = lax.fori_loop(0, n_dp, one, jnp.zeros((tokens, 128), F32))
        mean = jnp.sum(square, axis=1, keepdims=True) / float(feats)
        inv[...] = jnp.broadcast_to(lax.rsqrt(mean + 1e-06), (tokens, 128))

    def first(b, carry):
        misfits[0, :, cols(b)] = inj[:, cols(b)]
        add_gram(0, b)
        return carry

    lax.fori_loop(0, n_dp, first, 0)
    finish(0)

    for off in range(1, n_dp):
        inject_copy(off).wait_send()

    def iteration(k, carry):
        q = k - 1

        @pl.when(k == 1)
        def _():
            for copy in weight_copies((0, 1)):
                copy.wait()

        start = 0
        while start < hid:
            width = min(256, hid - start)
            tile = pl.ds(start, width)
            gate_val = jnp.dot(xg[...], w_gate[:, tile], preferred_element_type=F32)
            up_val = jnp.dot(xg[...], w_up[:, tile], preferred_element_type=F32)
            factor = inv[:, :1]
            gate_val = gate_val * factor
            up_val = up_val * factor
            hidden[:, tile] = (gate_val / (1.0 + jnp.exp(-gate_val)) * up_val).astype(BF16)
            start += width

        @pl.when(k == 1)
        def _():
            for copy in weight_copies((2,)):
                copy.wait()

        def pair_copy(t):
            return remote(
                pair_send.at[t], pair_recv.at[q, t], pair_ssem.at[t], pair_rsem.at[q, t],
                (sec, other),
            )

        def rs_copy(t):
            target = ((chip + 1 + t) % chips) * 2 + core
            return remote(
                rs_send.at[t], rs_recv.at[q, t], rs_ssem.at[t], rs_rsem.at[q, t],
                (sec, target),
            )

        def pass_on(t):
            pair_copy(t).wait_recv()
            rs_send[t] = (pair_mine[t] + pair_recv[q, t].astype(F32)).astype(BF16)
            rs_copy(t).start()

        def down(t, carry):
            aim = (chip + 1 + t) % chips
            theirs = jnp.dot(
                hidden[...], w_down[:, cols(2 * aim + 1 - core)], preferred_element_type=F32
            )
            pair_send[t] = theirs.astype(BF16)
            pair_copy(t).start()
            pair_mine[t] = jnp.dot(
                hidden[...], w_down[:, cols(2 * aim + core)], preferred_element_type=F32
            )

            @pl.when(t >= 1)
            def _():
                pass_on(t - 1)

            return carry

        lax.fori_loop(0, chips, down, 0)

        pair_copy(chips - 1).wait_recv()
        total = pair_mine[chips - 1] + pair_recv[q, chips - 1].astype(F32)

        def collect(t, value):
            rs_copy(t).wait_recv()
            return value + rs_recv[q, t].astype(F32)

        total = lax.fori_loop(0, chips - 1, collect, total)
        out_send[...] = (x[:, cols(me)] + total).astype(BF16)

        def ag_copy(b, slot, device):
            return remote(
                outs.at[q, b], outs.at[q, b], ag_ssem.at[slot], ag_rsem.at[q, b], device
            )

        z_copy = remote(out_send, outs.at[q, me], z_ssem, ag_rsem.at[q, me], (after, me))
        z_copy.start()

        def absorb(b):
            value = inj[:, cols(b)] + 0.5 * outs[q, b].astype(F32) - x[:, cols(b)]
            misfits[k, :, cols(b)] = value
            add_gram(k, b)

        z_copy.wait_recv()

        def spread(t, carry):
            ag_copy(me, t, (sec, ((chip + 1 + t) % chips) * 2 + core)).start()
            return carry

        lax.fori_loop(0, chips - 1, spread, 0)
        ag_copy(me, chips - 1, (sec, other)).start()
        absorb(me)

        def forward(t, carry):
            b = ((chip + chips - 1 - t) % chips) * 2 + core
            ag_copy(b, chips + t, (sec, other)).wait_recv()
            ag_copy(b, chips + t, (sec, other)).start()
            absorb(b)
            return carry

        lax.fori_loop(0, chips - 1, forward, 0)

        def last(t, carry):
            b = ((chip + chips - t) % chips) * 2 + 1 - core
            ag_copy(b, 0, (sec, other)).wait_recv()
            absorb(b)
            return carry

        lax.fori_loop(0, chips, last, 0)
        finish(k)

        def drain(t, carry):
            pair_copy(t).wait_send()
            return carry

        lax.fori_loop(0, chips, drain, 0)

        def drain_rs(t, carry):
            rs_copy(t).wait_send()
            return carry

        lax.fori_loop(0, chips - 1, drain_rs, 0)
        z_copy.wait_send()

        def drain_ag(t, carry):
            ag_copy(me, t, (sec, other)).wait_send()
            return carry

        lax.fori_loop(0, 2 * chips - 1, drain_ag, 0)
        return carry

    lax.fori_loop(1, ITERS, iteration, 0)
    out_ref[...] = x[pl.ds(pl.multiple_of(me * rows, rows), rows), :]


def solution(mesh):
    n_sec, n_dp = mesh.shape["section"], mesh.shape["dp"]
    chips = n_dp // 2

    def local(inject, w_gate, w_up, w_down, gain):
        rows, feats = inject.shape[1:]
        hid = w_gate.shape[2]
        tokens = rows * n_dp
        block = feats // n_dp
        rounds = ITERS - 1
        vmem = pl.BlockSpec(memory_space=pltpu.VMEM)
        hbm = pl.BlockSpec(memory_space=pl.ANY)
        dma = pltpu.SemaphoreType.DMA
        out, mixing = pl.pallas_call(
            functools.partial(kernel, n_sec, n_dp),
            out_shape=(
                jax.ShapeDtypeStruct((rows, feats), F32),
                jax.ShapeDtypeStruct((ITERS, HIST), F32),
            ),
            in_specs=[vmem, hbm, hbm, hbm, vmem],
            out_specs=(vmem, pl.BlockSpec(memory_space=pltpu.SMEM)),
            scratch_shapes=[
                pltpu.VMEM((feats, hid), BF16),
                pltpu.VMEM((feats, hid), BF16),
                pltpu.VMEM((hid, feats), BF16),
                pltpu.VMEM((n_dp, rows, feats), BF16),
                pltpu.VMEM((tokens, feats), F32),
                pltpu.VMEM((tokens, feats), F32),
                pltpu.VMEM((tokens, feats), BF16),
                pltpu.VMEM((tokens, 128), F32),
                pltpu.VMEM((tokens, hid), BF16),
                pltpu.VMEM((rounds, n_dp, tokens, block), BF16),
                pltpu.VMEM((HIST, tokens, feats), F32),
                pltpu.VMEM((HIST, 8, block), F32),
                pltpu.VMEM((HIST, HIST, 8, 128), F32),
                pltpu.VMEM((chips, tokens, block), BF16),
                pltpu.VMEM((rounds, chips, tokens, block), BF16),
                pltpu.VMEM((chips, tokens, block), F32),
                pltpu.VMEM((chips - 1, tokens, block), BF16),
                pltpu.VMEM((rounds, chips - 1, tokens, block), BF16),
                pltpu.VMEM((tokens, block), BF16),
                pltpu.SMEM((HIST,), F32),
                dma((3, ROW_CUTS)),
                dma((n_dp,)),
                dma((n_dp,)),
                dma((chips,)),
                dma((rounds, chips)),
                dma((chips,)),
                dma((rounds, chips)),
                dma,
                dma((2 * chips,)),
                dma((rounds, n_dp)),
            ],
            compiler_params=pltpu.CompilerParams(
                collective_id=0,
                has_side_effects=True,
                vmem_limit_bytes=67043328,
            ),
        )(inject[0], w_gate, w_up, w_down, gain)
        return out[None], mixing[None]

    placed = (
        P("section", "dp", None),
        P("section", None, "dp"),
        P("section", None, "dp"),
        P("section", "dp", None),
        P("section", None),
    )
    return jax.shard_map(
        local,
        mesh=mesh,
        in_specs=placed,
        out_specs=(P("section", "dp", None), P("section", None, None)),
        check_vma=False,
    )
```

time: 654 us -> 135 us (0.21); the launches traced: 642 us -> 134 us
  between operations: 189 us -> 0.64 us
  waiting for transfers between devices: 174 us -> 0 us
  matrix products: 129 us -> 0 us
  blocking collectives: 121 us -> 0 us
  Pallas kernels: 0 us -> 100 us
  local copies, waits for them, and re-layouts: 12.7 us -> 33.2 us
  other arithmetic: 9.55 us -> 0 us
    reduce_scatter x5 -> x0, waiting for transfers between devices: 157 us -> none  [local(): lax.psum_scatter(partials.astype(jnp.bfloat16), 'dp', scatter_dimension=0...]
    dot_general x20 -> x0, matrix products: 129 us -> none  [the longest x5 70.2 us: local(): partials = jnp.dot(hidden, down_local, preferred_element_type=jnp.float32)]
    pallas_call x0 -> x1, Pallas kernels: none -> 100 us  [local(): pl.pallas_call(functools.partial(kernel, n_sec, n_dp), out_shape=(jax.Sha...]
    psum x5 -> x0, blocking collectives: 67.6 us -> none  [local(): gram_matrix = lax.psum(local_gram, 'dp')]
    all_gather x5 -> x0, blocking collectives: 53.6 us -> none  [local(): segment = lax.all_gather(normed, 'dp', axis=0, tiled=True)]
    unnamed x6 -> x4, local copies, waits for them, and re-layouts: 0.64 us -> 33.2 us
    ppermute x5 -> x0, waiting for transfers between devices: 16.6 us -> none  [passed_along(): lax.ppermute(array, axis, [(i, (i + by) % peers) for i in range(peers)])]
    slice x15 -> x0, local copies, waits for them, and re-layouts: 10.2 us -> none  [the longest x10 6.88 us: solve_small(): entries = [[system[..., i, j] for j in range(count)] for i in range(count)]]
  transfers between devices with their start and end apart: 10 -> 0, of which waited for: 10 -> 0; matrix products, arithmetic and copies ran while one was open for 1% -> 0% of each run, Pallas kernels for 0% -> 0%
where the time goes in v1:
time: 135 us; the launch traced here: 134 us
  Pallas kernels  100 us (74%)
  local copies, waits for them, and re-layouts  33.2 us (25%)
    pallas_call x1, Pallas kernels, local(): pl.pallas_call(functools.partial(kernel, n_sec, n_dp), out_shape=(jax.Sha...  100 us
    unnamed x4, local copies, waits for them, and re-layouts  33.2 us

profile of v1, /device:TPU:1, one launch (start us, length us, event | category | flops | bytes accessed | tf_op | source)
XLA Modules:
  0.0 134.3 jit_solution(521893859965841435)
XLA Ops:
  0.6 15.2 %copy.7.gate_hbm = bf16[1,4096,1376]{2,1,0:T(8,128)(2,1)} copy(bf16[1,4096,1376]{1,2,0:T(8,128)(2,1)} %param.6) | data formatting | bytes 22544384 | tf_op args[1]
  15.9 15.2 %copy.8.up_hbm = bf16[1,4096,1376]{2,1,0:T(8,128)(2,1)} copy(bf16[1,4096,1376]{1,2,0:T(8,128)(2,1)} %param.7) | data formatting | bytes 22544384 | tf_op args[2]
  31.0 100.5 %shard_map.68 = (f32[8,4096]{1,0:T(8,128)}, f32[5,5]{1,0:T(8,128)}) custom-call(bf16[8,4096]{1,0:T(8,128)(2,1)} %bitcast.4, bf16[1,4096,1376]{2,1,0:T(8,128)(2,1)} %copy.7.gate_hbm, bf16[1,4096,1376]{2,1,0:T(8,128)(2,1)} %copy.8.up_hbm, bf16[1,1376,4096]{2,1,0:T(8,128)(2,1)} %down_hbm.1, f32[1,4096]{1,0:T(1,128)} %gain_ref.1), custom_call_target="tpu_custom_call" | custom-call | tf_op jit(solution)/shard_map/pallas_call | solution.py:329
  131.5 1.3 copy.9
  132.8 1.6 %copy.11 = f32[1,8,4096]{2,1,0:T(8,128)} copy(f32[1,8,4096]{2,1,0:T(8,128)} %bitcast.3) | data formatting | bytes 262144

commit v2 on v1

v2 whole, which is shorter than its diff:
```python
import functools

import jax
import jax.numpy as jnp
from jax import lax
from jax.experimental import pallas as pl
from jax.experimental.pallas import tpu as pltpu
from jax.sharding import PartitionSpec as P

ITERS = 5
HIST = 5
MESH = pl.DeviceIdType.MESH
F32 = jnp.float32
BF16 = jnp.bfloat16


def solve_small(entries, values):
    count = len(values)
    for p in range(count):
        for i in range(p + 1, count):
            factor = entries[i][p] / entries[p][p]
            for j in range(p, count):
                entries[i][j] = entries[i][j] - factor * entries[p][j]
            values[i] = values[i] - factor * values[p]
    answer = [None] * count
    for i in range(count - 1, -1, -1):
        accum = values[i]
        for j in range(i + 1, count):
            accum = accum - entries[i][j] * answer[j]
        answer[i] = accum / entries[i][i]
    return answer


def across(left, right):
    return lax.dot_general(
        left, right, (((1,), (1,)), ((), ())), preferred_element_type=F32
    )


def kernel(
    n_sec, n_dp,
    inj_ref, gate_hbm, up_hbm, down_hbm, gain_ref,
    out_ref, mix_ref,
    w_gate, w_up, w_down,
    inj_all, inj, x, gates, ups, inv, hidden,
    outs, misfits, acc, gram,
    pair_send, pair_recv, pair_mine, rs_send, rs_recv, out_send, mix_s,
    w_sem, inj_ssem, inj_rsem, pair_ssem, pair_rsem, rs_ssem, rs_rsem,
    z_ssem, ag_ssem, ag_rsem,
):
    sec = lax.axis_index("section")
    me = lax.axis_index("dp")
    chips = n_dp // 2
    chip = me // 2
    core = me % 2
    other = chip * 2 + 1 - core
    rows, feats = inj_ref.shape
    tokens = inj.shape[0]
    parts = pair_send.shape[0] // chips
    block = feats // (n_dp * parts)
    subs = n_dp * parts
    hid = hidden.shape[1]
    after = (sec + 1) % n_sec
    before = (sec + n_sec - 1) % n_sec

    def cols(b):
        return pl.ds(pl.multiple_of(b * block, block), block)

    def remote(src, dst, ssem, rsem, device):
        return pltpu.make_async_remote_copy(
            src_ref=src, dst_ref=dst, send_sem=ssem, recv_sem=rsem,
            device_id=device, device_id_type=MESH,
        )

    def weight_copy(a, b):
        src, dst = ((gate_hbm, w_gate), (up_hbm, w_up))[a]
        return pltpu.make_async_copy(src.at[0, :, cols(b)], dst.at[:, cols(b)], w_sem.at[a, b])

    def down_copy():
        return pltpu.make_async_copy(down_hbm.at[0], w_down, w_sem.at[2, 0])

    def fetch(b, carry):
        weight_copy(0, b).start()
        weight_copy(1, b).start()
        return carry

    lax.fori_loop(0, subs, fetch, 0)
    down_copy().start()

    barrier = pltpu.get_barrier_semaphore()
    for off in range(1, n_dp):
        pl.semaphore_signal(barrier, inc=1, device_id=(sec, (me + off) % n_dp), device_id_type=MESH)
    pl.semaphore_signal(barrier, inc=1, device_id=(after, me), device_id_type=MESH)
    pl.semaphore_signal(barrier, inc=1, device_id=(before, me), device_id_type=MESH)
    pl.semaphore_wait(barrier, n_dp + 1)

    def inject_copy(src, b, slot, device):
        return remote(src, inj_all.at[b], inj_ssem.at[slot], inj_rsem.at[b], (sec, device))

    for t in range(chips - 1):
        inject_copy(inj_ref, me, t, ((chip + 1 + t) % chips) * 2 + core).start()
    inject_copy(inj_ref, me, chips - 1, other).start()

    gram[...] = jnp.zeros_like(gram)
    acc[...] = jnp.zeros_like(acc)

    def place(b, values):
        inj[pl.ds(pl.multiple_of(b * rows, rows), rows), :] = values.astype(F32)

    place(me, inj_ref[...])
    inject_copy(inj_ref, other, 0, other).wait_recv()
    place(other, inj_all[other])
    for t in range(chips - 1):
        b = ((chip + chips - 1 - t) % chips) * 2 + core
        onward = inject_copy(inj_all.at[b], b, chips + t, other)
        onward.wait_recv()
        onward.start()
        place(b, inj_all[b])
    for t in range(chips - 1):
        b = ((chip + chips - 1 - t) % chips) * 2 + 1 - core
        inject_copy(inj_ref, b, 0, other).wait_recv()
        place(b, inj_all[b])

    def fold(values):
        return jnp.sum(values.reshape(tokens // 8, 8, block), axis=0)

    def add_gram(k, b):
        def one(j, carry):
            acc[j] = acc[j] + fold(misfits[k, :, cols(b)] * misfits[j, :, cols(b)])
            return carry

        lax.fori_loop(0, k + 1, one, 0)

    def project(k, b, image, fresh):
        scaled = (image * gain_ref[:, cols(b)]).astype(BF16)
        for kept, weights in ((gates, w_gate), (ups, w_up)):
            part = across(scaled, weights[:, cols(b)])
            if fresh:
                kept[k] = part
            else:
                kept[k] = kept[k] + part

    def finish(k):
        for j in range(HIST):
            total = jnp.sum(jnp.sum(acc[j], axis=0, keepdims=True), axis=1, keepdims=True)
            value = jnp.broadcast_to(total / float(tokens * feats), (8, 128))
            gram[k, j] = value
            gram[j, k] = value
        acc[...] = jnp.zeros_like(acc)
        live = [jnp.where(i <= k, 1.0, 0.0).astype(F32) for i in range(HIST)]
        trace = gram[0, 0]
        for i in range(1, HIST):
            trace = trace + gram[i, i]
        damp = 0.01 * trace / jnp.full((8, 128), k + 1, jnp.int32).astype(F32) + 1e-06
        system = [
            [
                gram[i, j] * (live[i] * live[j])
                + ((live[i] * damp + (1.0 - live[i])) if i == j else 0.0)
                for j in range(HIST)
            ]
            for i in range(HIST)
        ]
        beta = solve_small(system, [jnp.full((8, 128), live[i], F32) for i in range(HIST)])
        whole = beta[0]
        for i in range(1, HIST):
            whole = whole + beta[i]
        scale = jnp.float32(0.0)
        for i in range(HIST):
            weight = (beta[i] / whole)[0, 0]
            mix_ref[k, i] = weight
            mix_s[i] = weight
            scale = scale + weight

        def one(b, square):
            def slot(i, value):
                return value + (0.5 * mix_s[i]) * outs[i - 1, b].astype(F32)

            value = lax.fori_loop(1, k + 1, slot, scale * inj[:, cols(b)])
            x[:, cols(b)] = value
            squared = value * value
            for g in range(block // 128):
                square = square + squared[:, g * 128 : (g + 1) * 128]
            return square

        square = lax.fori_loop(0, subs, one, jnp.zeros((tokens, 128), F32))
        mean = jnp.sum(square, axis=1, keepdims=True) / float(feats)
        inv[...] = jnp.broadcast_to(lax.rsqrt(mean + 1e-06), (tokens, 128))

    def first(b, carry):
        misfits[0, :, cols(b)] = inj[:, cols(b)]
        add_gram(0, b)
        weight_copy(0, b).wait()
        weight_copy(1, b).wait()
        project(0, b, inj[:, cols(b)], False)
        return carry

    gates[0] = jnp.zeros_like(gates[0])
    ups[0] = jnp.zeros_like(ups[0])
    lax.fori_loop(0, subs, first, 0)
    finish(0)

    for t in range(2 * chips - 1):
        inject_copy(inj_ref, me, t, other).wait_send()

    def iteration(k, carry):
        q = k - 1

        start = 0
        while start < hid:
            width = min(256, hid - start)
            tile = pl.ds(start, width)

            def blend(i, pair):
                weight = mix_s[i]
                return pair[0] + weight * gates[i, :, tile], pair[1] + weight * ups[i, :, tile]

            empty = jnp.zeros((tokens, width), F32)
            gate_val, up_val = lax.fori_loop(0, k, blend, (empty, empty))
            factor = inv[:, :1]
            gate_val = gate_val * factor
            up_val = up_val * factor
            hidden[:, tile] = (gate_val / (1.0 + jnp.exp(-gate_val)) * up_val).astype(BF16)
            start += width

        @pl.when(k == 1)
        def _():
            down_copy().wait()

        def pair_copy(h, t):
            r = h * chips + t
            return remote(
                pair_send.at[r], pair_recv.at[q, r], pair_ssem.at[r], pair_rsem.at[q, r],
                (sec, other),
            )

        def rs_copy(h, t):
            r = h * (chips - 1) + t
            target = ((chip + 1 + t) % chips) * 2 + core
            return remote(
                rs_send.at[r], rs_recv.at[q, r], rs_ssem.at[r], rs_rsem.at[q, r],
                (sec, target),
            )

        def pass_on(h, t):
            pair_copy(h, t).wait_recv()
            r = h * chips + t
            both = pair_mine[r] + pair_recv[q, r].astype(F32)
            rs_send[h * (chips - 1) + t] = both.astype(BF16)
            rs_copy(h, t).start()

        for h in range(parts):

            def down(t, carry, h=h):
                aim = (chip + 1 + t) % chips
                r = h * chips + t
                theirs = jnp.dot(
                    hidden[...],
                    w_down[:, cols((2 * aim + 1 - core) * parts + h)],
                    preferred_element_type=F32,
                )
                pair_send[r] = theirs.astype(BF16)
                pair_copy(h, t).start()
                pair_mine[r] = jnp.dot(
                    hidden[...],
                    w_down[:, cols((2 * aim + core) * parts + h)],
                    preferred_element_type=F32,
                )

                @pl.when(t >= 1)
                def _():
                    pass_on(h, t - 1)

                return carry

            lax.fori_loop(0, chips, down, 0)

        def z_copy(h):
            u = me * parts + h
            return remote(out_send.at[h], outs.at[q, u], z_ssem.at[h], ag_rsem.at[q, u], (after, me))

        for h in range(parts):
            pair_copy(h, chips - 1).wait_recv()
            r = h * chips + chips - 1
            total = pair_mine[r] + pair_recv[q, r].astype(F32)

            def collect(t, value, h=h):
                rs_copy(h, t).wait_recv()
                return value + rs_recv[q, h * (chips - 1) + t].astype(F32)

            total = lax.fori_loop(0, chips - 1, collect, total)
            out_send[h] = (x[:, cols(me * parts + h)] + total).astype(BF16)
            z_copy(h).start()

        def ag_copy(u, slot, device):
            return remote(
                outs.at[q, u], outs.at[q, u], ag_ssem.at[slot], ag_rsem.at[q, u], device
            )

        def absorb(u, fresh=False):
            image = inj[:, cols(u)] + 0.5 * outs[q, u].astype(F32)
            misfits[k, :, cols(u)] = image - x[:, cols(u)]

            @pl.when(k < ITERS - 1)
            def _():
                project(k, u, image, fresh)

            add_gram(k, u)

        for h in range(parts):
            u = me * parts + h
            z_copy(h).wait_recv()

            def spread(t, carry, h=h, u=u):
                target = ((chip + 1 + t) % chips) * 2 + core
                ag_copy(u, h * 2 * chips + t, (sec, target)).start()
                return carry

            lax.fori_loop(0, chips - 1, spread, 0)
            ag_copy(u, h * 2 * chips + chips - 1, (sec, other)).start()
            absorb(u, h == 0)
            u = other * parts + h
            ag_copy(u, 0, (sec, other)).wait_recv()
            absorb(u)

        def forward(i, carry):
            h, t = i // (chips - 1), i % (chips - 1)
            u = (((chip + chips - 1 - t) % chips) * 2 + core) * parts + h
            onward = ag_copy(u, h * 2 * chips + chips + t, (sec, other))
            onward.wait_recv()
            onward.start()
            absorb(u)
            return carry

        lax.fori_loop(0, parts * (chips - 1), forward, 0)

        def last(i, carry):
            h, t = i // (chips - 1), i % (chips - 1)
            u = (((chip + chips - 1 - t) % chips) * 2 + 1 - core) * parts + h
            ag_copy(u, 0, (sec, other)).wait_recv()
            absorb(u)
            return carry

        lax.fori_loop(0, parts * (chips - 1), last, 0)
        finish(k)

        for h in range(parts):

            def drain(t, carry, h=h):
                pair_copy(h, t).wait_send()
                return carry

            lax.fori_loop(0, chips, drain, 0)

            def drain_rs(t, carry, h=h):
                rs_copy(h, t).wait_send()
                return carry

            lax.fori_loop(0, chips - 1, drain_rs, 0)
            z_copy(h).wait_send()

            def drain_ag(t, carry, h=h):
                ag_copy(me * parts + h, h * 2 * chips + t, (sec, other)).wait_send()
                return carry

            lax.fori_loop(0, 2 * chips - 1, drain_ag, 0)
        return carry

    lax.fori_loop(1, ITERS, iteration, 0)
    out_ref[...] = x[pl.ds(pl.multiple_of(me * rows, rows), rows), :]


def solution(mesh):
    n_sec, n_dp = mesh.shape["section"], mesh.shape["dp"]
    chips = n_dp // 2

    def local(inject, w_gate, w_up, w_down, gain):
        rows, feats = inject.shape[1:]
        hid = w_gate.shape[2]
        tokens = rows * n_dp
        parts = 1
        block = feats // (n_dp * parts)
        rounds = ITERS - 1
        vmem = pl.BlockSpec(memory_space=pltpu.VMEM)
        hbm = pl.BlockSpec(memory_space=pl.ANY)
        dma = pltpu.SemaphoreType.DMA
        out, mixing = pl.pallas_call(
            functools.partial(kernel, n_sec, n_dp),
            out_shape=(
                jax.ShapeDtypeStruct((rows, feats), F32),
                jax.ShapeDtypeStruct((ITERS, HIST), F32),
            ),
            in_specs=[vmem, hbm, hbm, hbm, vmem],
            out_specs=(vmem, pl.BlockSpec(memory_space=pltpu.SMEM)),
            scratch_shapes=[
                pltpu.VMEM((hid, feats), BF16),
                pltpu.VMEM((hid, feats), BF16),
                pltpu.VMEM((hid, feats), BF16),
                pltpu.VMEM((n_dp, rows, feats), BF16),
                pltpu.VMEM((tokens, feats), F32),
                pltpu.VMEM((tokens, feats), F32),
                pltpu.VMEM((rounds, tokens, hid), F32),
                pltpu.VMEM((rounds, tokens, hid), F32),
                pltpu.VMEM((tokens, 128), F32),
                pltpu.VMEM((tokens, hid), BF16),
                pltpu.VMEM((rounds, n_dp * parts, tokens, block), BF16),
                pltpu.VMEM((HIST, tokens, feats), F32),
                pltpu.VMEM((HIST, 8, block), F32),
                pltpu.VMEM((HIST, HIST, 8, 128), F32),
                pltpu.VMEM((parts * chips, tokens, block), BF16),
                pltpu.VMEM((rounds, parts * chips, tokens, block), BF16),
                pltpu.VMEM((parts * chips, tokens, block), F32),
                pltpu.VMEM((parts * (chips - 1), tokens, block), BF16),
                pltpu.VMEM((rounds, parts * (chips - 1), tokens, block), BF16),
                pltpu.VMEM((parts, tokens, block), BF16),
                pltpu.SMEM((HIST,), F32),
                dma((3, n_dp * parts)),
                dma((n_dp,)),
                dma((n_dp,)),
                dma((parts * chips,)),
                dma((rounds, parts * chips)),
                dma((parts * chips,)),
                dma((rounds, parts * chips)),
                dma((parts,)),
                dma((2 * chips * parts,)),
                dma((rounds, n_dp * parts)),
            ],
            compiler_params=pltpu.CompilerParams(
                collective_id=0,
                has_side_effects=True,
                vmem_limit_bytes=67043328,
            ),
        )(inject[0], jnp.swapaxes(w_gate, 1, 2), jnp.swapaxes(w_up, 1, 2), w_down, gain)
        return out[None], mixing[None]

    placed = (
        P("section", "dp", None),
        P("section", None, "dp"),
        P("section", None, "dp"),
        P("section", "dp", None),
        P("section", None),
    )
    return jax.shard_map(
        local,
        mesh=mesh,
        in_specs=placed,
        out_specs=(P("section", "dp", None), P("section", None, None)),
        check_vma=False,
    )
```

time: 135 us -> 110 us (0.81)
  local copies, waits for them, and re-layouts: 33.2 us -> 2.83 us
  Pallas kernels: 100 us -> 106 us
    unnamed x4 -> x2, local copies, waits for them, and re-layouts: 33.2 us -> 2.83 us
    pallas_call x1, Pallas kernels: 100 us -> 106 us  [local(): pl.pallas_call(functools.partial(kernel, n_sec, n_dp), out_shape=(jax.Sha...]
where the time goes in v2:
time: 110 us
  Pallas kernels  106 us (96%)
  local copies, waits for them, and re-layouts  2.83 us (3%)
    pallas_call x1, Pallas kernels, local(): pl.pallas_call(functools.partial(kernel, n_sec, n_dp), out_shape=(jax.Sha...  106 us
    unnamed x2, local copies, waits for them, and re-layouts  2.83 us

profile of v2, /device:TPU:1, one launch (start us, length us, event | category | flops | bytes accessed | tf_op | source)
XLA Modules:
  0.0 109.9 jit_solution(395797077020987697)
XLA Ops:
  0.6 106.4 %shard_map.68 = (f32[8,4096]{1,0:T(8,128)}, f32[5,5]{1,0:T(8,128)}) custom-call(bf16[8,4096]{1,0:T(8,128)(2,1)} %bitcast.8, bf16[1,1376,4096]{2,1,0:T(8,128)(2,1)} %bitcast.5, bf16[1,1376,4096]{2,1,0:T(8,128)(2,1)} %bitcast.6, bf16[1,1376,4096]{2,1,0:T(8,128)(2,1)} %down_hbm.1, f32[1,4096]{1,0:T(1,128)} %gain_ref.1), custom_call_target="tpu_custom_call" | custom-call | tf_op jit(solution)/shard_map/pallas_call | solution.py:386
  107.1 1.3 %copy.7 = f32[1,5,5]{2,0,1:T(1,128)} copy(f32[1,5,5]{2,1,0:T(8,128)} %bitcast.9) | data formatting | bytes 200
  108.4 1.6 %copy.9 = f32[1,8,4096]{2,1,0:T(8,128)} copy(f32[1,8,4096]{2,1,0:T(8,128)} %bitcast.7) | data formatting | bytes 262144

commit v3 on v2

--- a/solution.py
+++ b/solution.py
@@ -31,17 +31,11 @@
     return answer
 
 
-def across(left, right):
-    return lax.dot_general(
-        left, right, (((1,), (1,)), ((), ())), preferred_element_type=F32
-    )
-
-
 def kernel(
     n_sec, n_dp,
     inj_ref, gate_hbm, up_hbm, down_hbm, gain_ref,
     out_ref, mix_ref,
-    w_gate, w_up, w_down,
+    w_gate, w_up, w_down, stage,
     inj_all, inj, x, gates, ups, inv, hidden,
     outs, misfits, acc, gram,
     pair_send, pair_recv, pair_mine, rs_send, rs_recv, out_send, mix_s,
@@ -59,6 +53,7 @@
     parts = pair_send.shape[0] // chips
     block = feats // (n_dp * parts)
     subs = n_dp * parts
+    depth = stage.shape[1]
     hid = hidden.shape[1]
     after = (sec + 1) % n_sec
     before = (sec + n_sec - 1) % n_sec
@@ -73,8 +68,8 @@
         )
 
     def weight_copy(a, b):
-        src, dst = ((gate_hbm, w_gate), (up_hbm, w_up))[a]
-        return pltpu.make_async_copy(src.at[0, :, cols(b)], dst.at[:, cols(b)], w_sem.at[a, b])
+        src = (gate_hbm, up_hbm)[a]
+        return pltpu.make_async_copy(src.at[0, :, cols(b)], stage.at[a, b % depth], w_sem.at[a, b])
 
     def down_copy():
         return pltpu.make_async_copy(down_hbm.at[0], w_down, w_sem.at[2, 0])
@@ -84,7 +79,7 @@
         weight_copy(1, b).start()
         return carry
 
-    lax.fori_loop(0, subs, fetch, 0)
+    lax.fori_loop(0, depth, fetch, 0)
     down_copy().start()
 
     barrier = pltpu.get_barrier_semaphore()
@@ -103,6 +98,19 @@
 
     gram[...] = jnp.zeros_like(gram)
     acc[...] = jnp.zeros_like(acc)
+
+    def turn(b, carry):
+        for a, dst in enumerate((w_gate, w_up)):
+            weight_copy(a, b).wait()
+            dst[cols(b), :] = stage[a, b % depth].T
+
+        @pl.when(b + depth < subs)
+        def _():
+            fetch(b + depth, 0)
+
+        return carry
+
+    lax.fori_loop(0, subs // 2, turn, 0)
 
     def place(b, values):
         inj[pl.ds(pl.multiple_of(b * rows, rows), rows), :] = values.astype(F32)
@@ -116,6 +124,7 @@
         onward.wait_recv()
         onward.start()
         place(b, inj_all[b])
+    lax.fori_loop(subs // 2, subs, turn, 0)
     for t in range(chips - 1):
         b = ((chip + chips - 1 - t) % chips) * 2 + 1 - core
         inject_copy(inj_ref, b, 0, other).wait_recv()
@@ -134,7 +143,7 @@
     def project(k, b, image, fresh):
         scaled = (image * gain_ref[:, cols(b)]).astype(BF16)
         for kept, weights in ((gates, w_gate), (ups, w_up)):
-            part = across(scaled, weights[:, cols(b)])
+            part = jnp.dot(scaled, weights[cols(b), :], preferred_element_type=F32)
             if fresh:
                 kept[k] = part
             else:
@@ -189,8 +198,6 @@
     def first(b, carry):
         misfits[0, :, cols(b)] = inj[:, cols(b)]
         add_gram(0, b)
-        weight_copy(0, b).wait()
-        weight_copy(1, b).wait()
         project(0, b, inj[:, cols(b)], False)
         return carry
 
@@ -392,9 +399,10 @@
             in_specs=[vmem, hbm, hbm, hbm, vmem],
             out_specs=(vmem, pl.BlockSpec(memory_space=pltpu.SMEM)),
             scratch_shapes=[
+                pltpu.VMEM((feats, hid), BF16),
+                pltpu.VMEM((feats, hid), BF16),
                 pltpu.VMEM((hid, feats), BF16),
-                pltpu.VMEM((hid, feats), BF16),
-                pltpu.VMEM((hid, feats), BF16),
+                pltpu.VMEM((2, 3, hid, block), BF16),
                 pltpu.VMEM((n_dp, rows, feats), BF16),
                 pltpu.VMEM((tokens, feats), F32),
                 pltpu.VMEM((tokens, feats), F32),

time: 110 us -> 105 us (0.955)
  Pallas kernels: 106 us -> 101 us
    pallas_call x1, Pallas kernels: 106 us -> 101 us  [local(): pl.pallas_call(functools.partial(kernel, n_sec, n_dp), out_shape=(jax.Sha...]
where the time goes in v3:
time: 105 us; the launch traced here: 104 us
  Pallas kernels  101 us (96%)
  local copies, waits for them, and re-layouts  2.83 us (3%)
    pallas_call x1, Pallas kernels, local(): pl.pallas_call(functools.partial(kernel, n_sec, n_dp), out_shape=(jax.Sha...  101 us
    unnamed x2, local copies, waits for them, and re-layouts  2.83 us

profile of v3, /device:TPU:1, one launch (start us, length us, event | category | flops | bytes accessed | tf_op | source)
XLA Modules:
  0.0 104.5 jit_solution(17341107989499778437)
XLA Ops:
  0.6 101.0 %shard_map.68 = (f32[8,4096]{1,0:T(8,128)}, f32[5,5]{1,0:T(8,128)}) custom-call(bf16[8,4096]{1,0:T(8,128)(2,1)} %bitcast.8, bf16[1,1376,4096]{2,1,0:T(8,128)(2,1)} %bitcast.5, bf16[1,1376,4096]{2,1,0:T(8,128)(2,1)} %bitcast.6, bf16[1,1376,4096]{2,1,0:T(8,128)(2,1)} %down_hbm.1, f32[1,4096]{1,0:T(1,128)} %gain_ref.1), custom_call_target="tpu_custom_call" | custom-call | tf_op jit(solution)/shard_map/pallas_call | solution.py:393
  101.6 1.3 %copy.7 = f32[1,5,5]{2,0,1:T(1,128)} copy(f32[1,5,5]{2,1,0:T(8,128)} %bitcast.9) | data formatting | bytes 200
  102.9 1.6 %copy.9 = f32[1,8,4096]{2,1,0:T(8,128)} copy(f32[1,8,4096]{2,1,0:T(8,128)} %bitcast.7) | data formatting | bytes 262144
